TPU v7x, 32 devices: a whole 2x2x4 slice. The times are simulated.
32 devices in a mesh: space: 8 (over y, x, core), tm: 4 (over z).
Axes of the slice: x: 2, y: 2, z: 4, core: 2. Of those that a mesh axis runs over, the one named last changes fastest.
Arguments:
- links: float32 [4, 3, 2, 3, 3, 16, 4096], P('tm', None, None, None, None, 'space'), may hold values from -1 to 1, as said below
- propagator: float32 [2, 144, 16, 4096], P(None, 'tm', 'space'), may hold values from -6 to 6
- sink_time: int32 [1], replicated, may hold values from 0 to 16383
- src_time: int32 [1], replicated, may hold values from 0 to 16383
- src_site: int32 [1], replicated, may hold values from 0 to 65535
Outputs:
- fixed_links: float32 [4, 3, 2, 3, 3, 16, 4096], P('tm', None, None, None, None, 'space')
- wall: float32 [2, 144], replicated
Inputs may be any that keep to these rules, and one draw needn't show every extreme that they name: `links`: every link is a special unitary 3 x 3 matrix up to rounding.
All inputs are finite; a program needn't handle non-finite values.
Results may differ from a plain program's by a relative error of at most 0.0001.
Values sent between devices are 32-bit elements; how exact they have to be, the bound alone decides.
A program may use at most 128 MiB of HBM per device.

v0:
```python
import functools
import math

import jax
import jax.numpy as jnp
import numpy as np
from jax import lax
from jax.experimental import pallas as pl
from jax.experimental.pallas import tpu as pltpu
from jax.sharding import PartitionSpec as P

SC = 12
ITERS = 2
STEP = 0.08 / 16.0
PEAK = 12.0
LANES = 128
FIELDS = 8
EXACT = lax.Precision.HIGHEST
MESH = pl.DeviceIdType.MESH
VMEM = pl.BlockSpec(memory_space=pltpu.VMEM)
SMEM = pl.BlockSpec(memory_space=pltpu.SMEM)
LIMIT = 60 * 1024 * 1024


def real_basis(n):
    x = np.arange(n)
    rows, moment = [], []
    for k in range(n // 2 + 1):
        angle = 2.0 * np.pi * ((k * x) % n) / n
        square = 4.0 * np.sin(np.pi * k / n) ** 2
        if k == 0 or 2 * k == n:
            rows.append(np.cos(angle) / np.sqrt(n))
            moment.append(square)
        else:
            rows.append(np.cos(angle) * np.sqrt(2.0 / n))
            rows.append(np.sin(angle) * np.sqrt(2.0 / n))
            moment += [square, square]
    return np.array(rows), np.array(moment)


def halves(m):
    high = m.astype(jnp.bfloat16)
    return high, (m - high.astype(np.float64)).astype(jnp.bfloat16)


def plane_matrices(q):
    n = q.shape[0]
    zero = np.zeros((n, n))
    right = np.block([[q.T, zero, zero, q.T], [zero, q.T, q.T, zero]])
    even, odd = q[0::2], q[1::2]
    left = np.block([[even[:, 0::2], even[:, 1::2]], [odd[:, 1::2], odd[:, 0::2]]])
    high, low = halves(right)
    right = np.concatenate([high, high, low], axis=0)
    high, low = halves(left)
    return right, np.concatenate([high, high, low], axis=1)


def triple(x, axis):
    high = x.astype(jnp.bfloat16)
    low = (x - high.astype(jnp.float32)).astype(jnp.bfloat16)
    return jnp.concatenate([high, low, high], axis=axis)


def dot(a, b):
    return jnp.dot(a, b, preferred_element_type=jnp.float32)


def plane_transform(slabs, right, left):
    rows = slabs[0].shape[0]
    wide = dot(triple(jnp.concatenate(slabs, axis=0), 1), right)
    count = len(slabs)
    straight = [wide[i * rows : (i + 1) * rows, :LANES] for i in range(count)]
    swapped = [wide[i * rows : (i + 1) * rows, LANES:] for i in range(count)]
    tall = jnp.concatenate(
        [jnp.concatenate(straight, axis=1), jnp.concatenate(swapped, axis=1)], axis=0
    )
    both = dot(left, triple(tall, 0))
    low = lax.broadcasted_iota(jnp.int32, (rows, LANES), 1) < LANES // 2
    return [
        jnp.where(
            low,
            both[:rows, i * LANES : (i + 1) * LANES],
            both[rows:, i * LANES : (i + 1) * LANES],
        )
        for i in range(count)
    ]


def lane_of(shape):
    return lax.broadcasted_iota(jnp.int32, shape, 1)


def y_behind(v):
    half = LANES // 2
    r = pltpu.roll(v, half, 1)
    return jnp.where(lane_of(v.shape) < half, pltpu.roll(r, 1, 0), r)


def y_ahead(v):
    half = LANES // 2
    r = pltpu.roll(v, half, 1)
    return jnp.where(lane_of(v.shape) < half, r, pltpu.roll(r, v.shape[0] - 1, 0))


def z_behind(v):
    half = LANES // 2
    edge = lane_of(v.shape) % half == 0
    return jnp.where(edge, pltpu.roll(v, half + 1, 1), pltpu.roll(v, 1, 1))


def z_ahead(v):
    half = LANES // 2
    edge = lane_of(v.shape) % half == half - 1
    return jnp.where(edge, pltpu.roll(v, half - 1, 1), pltpu.roll(v, LANES - 1, 1))


PAIRS = ((0, 1), (0, 2), (1, 2))


def project(get, f):
    if f < 6:
        a, b = PAIRS[f % 3]
        if f < 3:
            return 0.5 * (get(0, a, b) - get(0, b, a))
        return 0.5 * (get(1, a, b) + get(1, b, a))
    diag = [get(1, a, a) for a in range(3)]
    return diag[f - 6] - (diag[0] + diag[1] + diag[2]) * (1.0 / 3.0)


def cmul(a, b):
    return (a[0] * b[0] - a[1] * b[1], a[0] * b[1] + a[1] * b[0])


def exponential(fields):
    v = [STEP * f for f in fields]
    h0, h1 = v[6], v[7]
    h2 = -(h0 + h1)
    h01, h02, h12 = (v[3], -v[0]), (v[4], -v[1]), (v[5], -v[2])
    n01 = h01[0] * h01[0] + h01[1] * h01[1]
    n02 = h02[0] * h02[0] + h02[1] * h02[1]
    n12 = h12[0] * h12[0] + h12[1] * h12[1]
    c = 0.5 * (h0 * h0 + h1 * h1 + h2 * h2) + n01 + n02 + n12
    prod = cmul(h01, h12)
    triple = prod[0] * h02[0] + prod[1] * h02[1]
    d = h0 * h1 * h2 + 2.0 * triple - h0 * n12 - h1 * n02 - h2 * n01
    cd, cc, dd = c * d, c * c, d * d
    f0 = (1.0 - dd * (1 / 720), cd * (1 / 120) - d * (1 / 6))
    f1 = (d * (1 / 24) - cd * (1 / 360), 1.0 - c * (1 / 6) + cc * (1 / 120))
    f2 = (c * (1 / 24) - 0.5 - cc * (1 / 720), d * (1 / 120))
    for _ in range(3):
        s00, s01, s02 = cmul(f0, f0), cmul(f0, f1), cmul(f0, f2)
        s11, s12, s22 = cmul(f1, f1), cmul(f1, f2), cmul(f2, f2)
        f0 = tuple(s00[i] + 2.0 * d * s12[i] for i in range(2))
        f1 = tuple(2.0 * (s01[i] + c * s12[i]) + d * s22[i] for i in range(2))
        f2 = tuple(s11[i] + 2.0 * s02[i] + c * s22[i] for i in range(2))
    conj = lambda x: (x[0], -x[1])
    mixed = cmul(h02, conj(h12))
    q01 = (mixed[0] - h2 * h01[0], mixed[1] - h2 * h01[1])
    q02 = (prod[0] - h1 * h02[0], prod[1] - h1 * h02[1])
    mixed = cmul(conj(h01), h02)
    q12 = (mixed[0] - h0 * h12[0], mixed[1] - h0 * h12[1])
    diag = ((h0, h0 * h0 + n01 + n02), (h1, h1 * h1 + n01 + n12), (h2, h2 * h2 + n02 + n12))
    gauge = [[None] * 3 for _ in range(3)]
    for a in range(3):
        h, q = diag[a]
        gauge[a][a] = tuple(f0[i] + f1[i] * h + f2[i] * q for i in range(2))
    for a, b, h, q in ((0, 1, h01, q01), (0, 2, h02, q02), (1, 2, h12, q12)):
        x, y = cmul(f1, h), cmul(f2, q)
        gauge[a][b] = (x[0] + y[0], x[1] + y[1])
        x, y = cmul(f1, conj(h)), cmul(f2, conj(q))
        gauge[b][a] = (x[0] + y[0], x[1] + y[1])
    return gauge


def matmul3(left, right, adjoint=False):
    out = [[None] * 3 for _ in range(3)]
    for a in range(3):
        for b in range(3):
            re = im = None
            for k in range(3):
                xr, xi = left[a][k]
                yr, yi = right[b][k] if adjoint else right[k][b]
                if adjoint:
                    r, i = xr * yr + xi * yi, xi * yr - xr * yi
                else:
                    r, i = xr * yr - xi * yi, xr * yi + xi * yr
                re, im = (r, i) if re is None else (re + r, im + i)
            out[a][b] = (re, im)
    return out


def at(part, a, b):
    return part * 9 + a * 3 + b


class Swap:
    def __init__(self, size, send, recv, send_sem, recv_sem):
        self.size, self.send, self.recv = size, send, recv
        self.send_sem, self.recv_sem = send_sem, recv_sem
        self.me = lax.axis_index("space")

    def copy(self, g, off):
        peer = lax.rem(self.me + off, self.size)
        return pltpu.make_async_remote_copy(
            src_ref=self.send.at[g, peer],
            dst_ref=self.recv.at[g, self.me],
            send_sem=self.send_sem.at[g, off],
            recv_sem=self.recv_sem.at[g, off],
            device_id={"space": peer},
            device_id_type=MESH,
        )

    def start(self, g):
        for off in range(1, self.size):
            self.copy(g, off).start()
        self.recv[g, self.me] = self.send[g, self.me]

    def arrive(self, g):
        for off in range(1, self.size):
            self.copy(g, off).wait_recv()

    def drain(self):
        for g in range(self.send.shape[0]):
            for off in range(1, self.size):
                self.copy(g, off).wait_send()


class Relay:
    def __init__(self, size, root, own, up, down, sems):
        self.size, self.root, self.own = size, root, own
        self.up, self.down = up, down
        self.sems = sems
        self.me = lax.axis_index("tm")
        self.deep = min(size, 4)

    def hop(self, k, rise):
        buffer = self.up if rise else self.down
        base = 0 if rise else 2
        step = 1 if rise else self.size - 1
        return pltpu.make_async_remote_copy(
            src_ref=buffer.at[k],
            dst_ref=buffer.at[k],
            send_sem=self.sems.at[base, k],
            recv_sem=self.sems.at[base + 1, k],
            device_id={"tm": lax.rem(self.me + step, self.size)},
            device_id_type=MESH,
        )

    def step(self, k, h):
        for rise in (True, False):
            place = self.me if rise else self.size - 1 - self.me
            last = h == self.deep - 1
            here = (place >= h) if last else (place == h)
            buffer = self.up if rise else self.down
            parts = buffer.shape[1]

            @pl.when(here)
            def _():
                if h == 0:
                    for j in range(parts):
                        buffer[k, j] = self.own(k, j)
                else:
                    self.hop(k, rise).wait_recv()
                    mine = jnp.broadcast_to(self.root, buffer.shape[2:]) == self.me
                    for j in range(parts):
                        buffer[k, j] = jnp.where(mine, self.own(k, j), buffer[k, j])
                if not last:
                    self.hop(k, rise).start()
                elif self.size > self.deep:

                    @pl.when(place < self.size - 1)
                    def _():
                        self.hop(k, rise).start()

    def drain(self):
        for k in range(self.up.shape[0]):

            @pl.when(self.me < self.size - 1)
            def _():
                self.hop(k, True).wait_send()

            @pl.when(self.me > 0)
            def _():
                self.hop(k, False).wait_send()

    def value(self, k, j, band):
        own = self.own(k, j, band)
        root = jnp.broadcast_to(self.root, own.shape)
        other = jnp.where(root < self.me, self.up[k, j, band, :], self.down[k, j, band, :])
        return jnp.where(root == self.me, own, other)


def greet(axis, offsets, sizes):
    barrier = pltpu.get_barrier_semaphore()
    me = lax.axis_index(axis)
    for off in offsets:
        peer = lax.rem(me + off, sizes[axis])
        pl.semaphore_signal(barrier, inc=1, device_id={axis: peer}, device_id_type=MESH)
    return len(offsets)


class Plan:
    def __init__(self, sizes, planes, rows, basis, moment):
        self.sizes, self.planes, self.rows = sizes, planes, rows
        self.basis, self.moment = basis, moment
        self.size = sizes["space"]
        self.ratio = 8 * self.size // rows
        self.groups = FIELDS // self.ratio
        assert self.ratio * rows == 8 * self.size and self.groups * self.ratio == FIELDS
        self.levels = sorted(set(np.round(moment, 9)))
        self.chunk = (self.groups, self.size, planes + 1, 8, LANES)
        self.slab = (FIELDS * (planes + 1), rows, LANES)

    def fields(self, g):
        return range(g * self.ratio, (g + 1) * self.ratio)

    def exchange_scratch(self):
        sems = pltpu.SemaphoreType.DMA((self.groups, self.size))
        return [pltpu.VMEM(self.chunk, jnp.float32)] * 4 + [
            pltpu.VMEM((len(self.levels), 8, LANES), jnp.float32)
        ] + [sems] * 4


def weigh(plan, yz_ref, weight_ref):
    block = lax.div(lax.axis_index("space"), plan.ratio)
    yz = yz_ref[pl.ds(pl.multiple_of(block * 8, 8), 8), :]
    for index, level in enumerate(plan.levels):
        p2 = yz + float(level)
        if level == 0.0:
            weight = jnp.where(p2 > 0.0, PEAK / jnp.where(p2 > 0.0, p2, 1.0), 0.0)
        else:
            weight = PEAK / p2
        weight_ref[index] = weight


def forward(plan, u, g, right, left, send_ref):
    planes = plan.planes
    slabs = []
    for f in plan.fields(g):
        before = None
        for p in range(planes):
            x, y, z = (
                project(lambda part, a, b, i=i: u(i, part, a, b, p), f) for i in range(3)
            )
            value = (y_behind(y) - y + z_behind(z) - z) - x
            slabs.append(value if before is None else value + before)
            before = x
        slabs.append(before)
    done = plane_transform(slabs, right, left)
    for index, slab in enumerate(done):
        i, p = divmod(index, planes + 1)
        for block in range(plan.rows // 8):
            send_ref[g, block * plan.ratio + i, p] = slab[block * 8 : block * 8 + 8, :]


def backward(plan, g, right, left, recv_ref, slab_ref):
    slabs = []
    for i in range(plan.ratio):
        for p in range(plan.planes + 1):
            slabs.append(
                jnp.concatenate(
                    [recv_ref[g, b * plan.ratio + i, p] for b in range(plan.rows // 8)],
                    axis=0,
                )
            )
    base = g * plan.ratio * (plan.planes + 1)
    for index, slab in enumerate(plane_transform(slabs, right, left)):
        slab_ref[base + index] = slab


def across(plan, g, recv_ref, weight_ref, send_ref):
    planes, count, basis = plan.planes, plan.size, plan.basis
    n = basis.shape[0]
    v = []
    for s in range(count):
        for p in range(planes):
            value = recv_ref[g, s, p]
            if p == 0:
                value = value + recv_ref[g, (s - 1) % count, planes]
            v.append(value)
    half = range(1, (n + 1) // 2)
    even = {0: v[0]}
    odd = {}
    if n % 2 == 0:
        even[n // 2] = v[n // 2]
    for x in half:
        even[x] = v[x] + v[n - x]
        odd[x] = v[x] - v[n - x]
    back_even = {x: None for x in even}
    back_odd = {x: None for x in odd}
    for k in range(n):
        is_sine = abs(basis[k, 0]) < 1e-9
        source, target = (odd, back_odd) if is_sine else (even, back_even)
        mode = None
        for x in source:
            term = float(basis[k, x]) * source[x]
            mode = term if mode is None else mode + term
        mode = mode * weight_ref[plan.levels.index(np.round(plan.moment[k], 9))]
        for x in target:
            term = float(basis[k, x]) * mode
            target[x] = term if target[x] is None else target[x] + term
    out = [None] * n
    for x in back_even:
        out[x] = back_even[x]
    for x in half:
        out[x] = back_even[x] + back_odd[x]
        out[n - x] = back_even[x] - back_odd[x]
    for d in range(count):
        for p in range(planes + 1):
            send_ref[g, d, p] = out[(d * planes + p) % n]


def first_kernel(
    plan, links_ref, right_ref, left_ref, back_ref, turn_ref, yz_ref, slab_ref,
    send_one, recv_one, send_two, recv_two, weight_ref, *sems,
):
    planes, rows = plan.planes, plan.rows
    total = greet("space", range(1, plan.size), plan.sizes)
    one = Swap(plan.size, send_one, recv_one, sems[0], sems[1])
    two = Swap(plan.size, send_two, recv_two, sems[2], sems[3])

    def u(i, part, a, b, p):
        return links_ref[i * 18 + at(part, a, b), pl.ds(p, rows, planes), :]

    for g in range(plan.groups):
        forward(plan, u, g, right_ref[...], left_ref[...], send_one)
        if g == 0:
            pl.semaphore_wait(pltpu.get_barrier_semaphore(), total)
        one.start(g)
    weigh(plan, yz_ref, weight_ref)
    for g in range(plan.groups):
        one.arrive(g)
        across(plan, g, recv_one, weight_ref, send_two)
        two.start(g)
    for g in range(plan.groups):
        two.arrive(g)
        backward(plan, g, back_ref[...], turn_ref[...], recv_two, slab_ref)
    one.drain()
    two.drain()


def gauge_of(slab_ref, planes, gauge_ref):
    rows = gauge_ref.shape[2]

    for p in range(planes + 1):

        @pl.loop(0, rows // 8)
        def _(j):
            band = pl.ds(pl.multiple_of(j * 8, 8), 8)
            g = exponential([slab_ref[f * (planes + 1) + p, band, :] for f in range(FIELDS)])
            for a in range(3):
                for b in range(3):
                    for part in range(2):
                        gauge_ref[at(part, a, b), p, band, :] = g[a][b][part]


def shift_all(planes, gauge_ref, ahead_ref):
    for e in range(18):
        for p in range(planes):
            ahead_ref[e, p] = y_ahead(gauge_ref[e, p])
            ahead_ref[18 + e, p] = z_ahead(gauge_ref[e, p])


def rotate_plane(get_band, put_band, p, gauge_ref, ahead_ref):
    rows = gauge_ref.shape[2]

    @pl.loop(0, rows // 8)
    def _(j):
        start = pl.multiple_of(j * 8, 8)
        band = pl.ds(start, 8)
        for i in range(3):
            g = [
                [tuple(gauge_ref[at(r, a, b), p, band, :] for r in range(2)) for b in range(3)]
                for a in range(3)
            ]
            u = [
                [tuple(get_band(i, r, a, b, p, j) for r in range(2)) for b in range(3)]
                for a in range(3)
            ]
            if i == 0:
                source = lambda r, a, b: gauge_ref[at(r, a, b), p + 1, band, :]
            else:
                source = lambda r, a, b: ahead_ref[(i - 1) * 18 + at(r, a, b), p, band, :]
            ahead = [
                [tuple(source(r, a, b) for r in range(2)) for b in range(3)]
                for a in range(3)
            ]
            out = matmul3(matmul3(g, u), ahead, adjoint=True)
            for a in range(3):
                for b in range(3):
                    for r in range(2):
                        put_band(i, r, a, b, p, j, out[a][b][r])


def relay_order(chunks, deep):
    steps = [(k, h) for k in range(chunks) for h in range(1, deep)]
    return sorted(steps, key=lambda s: 1.4 * (s[0] + s[1]) + 2.1 * s[1])


def second_kernel(
    plan, root_ref, links_ref, slab_one, right_ref, left_ref, back_ref, turn_ref, yz_ref,
    out_ref, slab_two, spread_ref,
    send_one, recv_one, send_two, recv_two, weight_ref, sem_a, sem_b, sem_c, sem_d,
    gauge_ref, ahead_ref, up_ref, down_ref, relay_sems,
):
    planes, rows, sizes = plan.planes, plan.rows, plan.sizes
    total = greet("space", range(1, plan.size), sizes)
    total += greet("tm", (1, sizes["tm"] - 1), sizes)
    one = Swap(plan.size, send_one, recv_one, sem_a, sem_b)
    two = Swap(plan.size, send_two, recv_two, sem_c, sem_d)

    def own(k, j, band=slice(None)):
        i, p = divmod(j, planes)
        return slab_one[(k * plan.ratio + i) * (planes + 1) + p, band, :]

    relay = Relay(sizes["tm"], root_ref[0], own, up_ref, down_ref, relay_sems)
    gauge_of(slab_one, planes, gauge_ref)
    shift_all(planes, gauge_ref, ahead_ref)

    def get(i, r, a, b, p, j):
        return links_ref[i * 18 + at(r, a, b), pl.ds(j * 8 * planes + p, 8, planes), :]

    def put(i, r, a, b, p, j, value):
        out_ref[i * 18 + at(r, a, b), p, pl.ds(pl.multiple_of(j * 8, 8), 8), :] = value

    for p in range(planes):
        rotate_plane(get, put, p, gauge_ref, ahead_ref)

    def u(i, part, a, b, p):
        return out_ref[i * 18 + at(part, a, b), p]

    steps = relay_order(plan.groups, relay.deep)

    def advance(count):
        for _ in range(count):
            if steps:
                relay.step(*steps.pop(0))

    pl.semaphore_wait(pltpu.get_barrier_semaphore(), total)
    for k in range(plan.groups):
        relay.step(k, 0)
    for g in range(plan.groups):
        forward(plan, u, g, right_ref[...], left_ref[...], send_one)
        one.start(g)
    weigh(plan, yz_ref, weight_ref)
    advance(3)
    for g in range(plan.groups):
        one.arrive(g)
        across(plan, g, recv_one, weight_ref, send_two)
        two.start(g)
        advance(1)
    for g in range(plan.groups):
        advance(1)
        two.arrive(g)
        backward(plan, g, back_ref[...], turn_ref[...], recv_two, slab_two)
    advance(len(steps))
    for k in range(plan.groups):
        for j in range(plan.ratio * planes):
            i, p = divmod(j, planes)
            spread_ref[(k * plan.ratio + i) * planes + p] = relay.value(k, j, slice(None))
    one.drain()
    two.drain()
    relay.drain()


class Gather:
    def __init__(self, sizes, axes, target, send, recv):
        self.axes, self.target, self.send, self.recv = axes, target, send, recv
        me = [lax.axis_index(axis) for axis in axes]
        extent = [sizes[axis] for axis in axes]
        slot = 0
        for index, size in zip(me, extent):
            slot = slot * size + index
        self.slot = slot
        self.peers = []
        for flat in range(1, math.prod(extent)):
            rest, peer = flat, {}
            for axis, index, size in reversed(list(zip(axes, me, extent))):
                peer[axis] = lax.rem(index + rest % size, size)
                rest //= size
            self.peers.append((flat, peer))

    def greet(self):
        barrier = pltpu.get_barrier_semaphore()
        for _, peer in self.peers:
            pl.semaphore_signal(barrier, inc=1, device_id=peer, device_id_type=MESH)
        return len(self.peers)

    def run(self, source):
        copies = []
        for flat, peer in self.peers:
            copies.append(
                pltpu.make_async_remote_copy(
                    src_ref=source,
                    dst_ref=self.target.at[self.slot],
                    send_sem=self.send.at[flat],
                    recv_sem=self.recv.at[flat],
                    device_id=peer,
                    device_id_type=MESH,
                )
            )
            copies[-1].start()
        self.target[self.slot] = source[...]
        for copy in copies:
            copy.wait()


def third_kernel(
    plan, stages, scalar_ref, lattice_ref, slab_one, slab_two, spread_ref, prop_ref,
    out_ref, table_ref,
    gauge_ref, ahead_ref, up_ref, down_ref, relay_sems, acc_ref, sum_ref, row_ref, *gathers,
):
    planes, rows, sizes = plan.planes, plan.rows, plan.sizes
    root, present, plane, line, lane = (scalar_ref[i] for i in range(5))
    stages = [
        Gather(sizes, axes, *gathers[3 * i : 3 * i + 3]) for i, axes in enumerate(stages)
    ]
    total = sum(stage.greet() for stage in stages)

    def own(k, j, band=slice(None)):
        i, p = divmod(j, planes)
        return slab_two[(k * plan.ratio + i) * (planes + 1) + p, band, :]

    relay = Relay(sizes["tm"], root, own, up_ref, down_ref, relay_sems)
    pl.semaphore_wait(pltpu.get_barrier_semaphore(), total)
    for k in range(plan.groups):
        relay.step(k, 0)
    steps = relay_order(plan.groups, relay.deep)

    def advance(count):
        for _ in range(count):
            if steps:
                relay.step(*steps.pop(0))

    gauge_of(slab_two, planes, gauge_ref)
    shift_all(planes, gauge_ref, ahead_ref)

    def get(i, r, a, b, p, j):
        return lattice_ref[i * 18 + at(r, a, b), p, pl.ds(pl.multiple_of(j * 8, 8), 8), :]

    def put(i, r, a, b, p, j, value):
        out_ref[i * 18 + at(r, a, b), pl.ds(j * 8 * planes + p, 8, planes), :] = value

    for p in range(planes):
        rotate_plane(get, put, p, gauge_ref, ahead_ref)
        advance(2)
    acc_ref[...] = jnp.zeros_like(acc_ref)
    sum_ref[...] = jnp.zeros_like(sum_ref)
    spot = (lax.broadcasted_iota(jnp.int32, (rows, LANES), 0) == line) & (
        lax.broadcasted_iota(jnp.int32, (rows, LANES), 1) == lane
    )

    def pick(ref, f):
        value = jnp.zeros((1, 1), jnp.float32)
        for p in range(planes):
            here = spot & (plane == p)
            entry = ref[f * (planes + 1) + p]
            value = value + jnp.sum(jnp.where(here, entry, 0.0), keepdims=True)
        return jnp.broadcast_to(value, (8, LANES))

    anchor = matmul3(
        exponential([pick(slab_two, f) for f in range(FIELDS)]),
        exponential([pick(slab_one, f) for f in range(FIELDS)]),
    )
    pairs = prop_ref.shape[0] // 2
    first = lane_of((1, LANES)) == 0
    for r in range(2):
        for a in range(3):
            for b in range(3):
                e = 2 * pairs + at(r, a, b)
                sum_ref[e : e + 1, :] = jnp.where(
                    first & (present > 0), anchor[a][b][r][0:1, :], 0.0
                )
    advance(len(steps))

    for p in range(planes):

        @pl.loop(0, rows // 8)
        def _(j):
            band = pl.ds(pl.multiple_of(j * 8, 8), 8)
            one = exponential([spread_ref[f * planes + p, band, :] for f in range(FIELDS)])
            two = exponential(
                [
                    relay.value(f // plan.ratio, (f % plan.ratio) * planes + p, band)
                    for f in range(FIELDS)
                ]
            )
            t = matmul3(two, one)
            for q in range(pairs // 3):
                s = [
                    tuple(
                        prop_ref[r * pairs + q * 3 + k, pl.ds(j * 8 * planes + p, 8, planes), :]
                        for r in range(2)
                    )
                    for k in range(3)
                ]
                for a in range(3):
                    re = im = None
                    for k in range(3):
                        x = cmul(t[a][k], s[k])
                        re, im = x if re is None else (re + x[0], im + x[1])
                    acc_ref[q * 3 + a] += re
                    acc_ref[pairs + q * 3 + a] += im

    for e in range(2 * pairs):
        sum_ref[e : e + 1, :] = jnp.sum(acc_ref[e], axis=0, keepdims=True)
    row_ref[...] = lax.dot_general(
        jnp.ones((8, LANES), jnp.float32),
        sum_ref[...],
        (((1,), (1,)), ((), ())),
        precision=EXACT,
        preferred_element_type=jnp.float32,
    )[0:1, :]
    space, times = sizes["space"], sizes["tm"]
    stages[0].run(row_ref)
    if len(stages) == 1:
        for t in range(times):
            value = stages[0].target[t]
            for s in range(1, space):
                value = value + stages[0].target[s * times + t]
            table_ref[t : t + 1, :] = value
    else:
        value = stages[0].target[0]
        for s in range(1, space):
            value = value + stages[0].target[s]
        row_ref[...] = value
        stages[1].run(row_ref)
        for t in range(times):
            table_ref[t : t + 1, :] = stages[1].target[t]
    relay.drain()


def call(kernel, outs, scratch, args, collective_id, smem=0):
    return pl.pallas_call(
        kernel,
        out_shape=[jax.ShapeDtypeStruct(s, jnp.float32) for s in outs],
        in_specs=[SMEM] * smem + [VMEM] * (len(args) - smem),
        out_specs=[VMEM] * len(outs),
        scratch_shapes=[
            pltpu.VMEM(s, jnp.float32) if isinstance(s, tuple) else s for s in scratch
        ],
        compiler_params=pltpu.CompilerParams(
            collective_id=collective_id, has_side_effects=True, vmem_limit_bytes=LIMIT
        ),
    )(*args)


def body(sizes, links, propagator, sink_time, src_time, src_site):
    space, times = sizes["space"], sizes["tm"]
    planes, area = links.shape[5], links.shape[6]
    side = math.isqrt(area)
    wide = planes * space
    rows = area // LANES
    assert side * 2 == LANES and rows % 8 == 0

    basis, moment = real_basis(side)
    right, left = plane_matrices(basis)
    back, turn = plane_matrices(basis.T)
    x_basis, x_moment = real_basis(wide)
    yz = (moment.reshape(rows, 2, 1) + moment[None, None, :]).reshape(rows, LANES)
    yz = yz.astype(np.float32)
    plan = Plan(sizes, planes, rows, x_basis, x_moment)

    def fold(x):
        lead = x.shape[:-2]
        x = x.reshape(lead + (planes, rows, LANES))
        return jnp.swapaxes(x, -3, -2).reshape((-1, rows * planes, LANES))

    linked = fold(links[0])
    field = (FIELDS * planes, rows, LANES)
    gauge = (18, planes + 1, rows, LANES)
    ahead = (36, planes, rows, LANES)
    split = (54, planes, rows, LANES)
    spread = (plan.groups, plan.ratio * planes, rows, LANES)
    relay_sems = pltpu.SemaphoreType.DMA((4, plan.groups))

    site = src_site[0]
    space_index = lax.axis_index("space")
    time_index = lax.axis_index("tm")
    plane = site // area - space_index * planes
    column = site % area
    present = (src_time[0] % times == time_index) & (plane >= 0) & (plane < planes)
    scalars = jnp.stack(
        [
            sink_time[0] % times,
            present.astype(jnp.int32),
            plane,
            column // LANES,
            column % LANES,
        ]
    )

    (slab_one,) = call(
        functools.partial(first_kernel, plan),
        [plan.slab],
        plan.exchange_scratch(),
        [linked, right, left, back, turn, yz],
        0,
    )
    lattice, slab_two, spread_one = call(
        functools.partial(second_kernel, plan),
        [split, plan.slab, field],
        plan.exchange_scratch() + [gauge, ahead, spread, spread, relay_sems],
        [scalars, linked, slab_one, right, left, back, turn, yz],
        1,
        smem=1,
    )
    pairs = propagator.shape[1]
    assert 2 * pairs + 18 <= LANES
    stages = [("space", "tm")] if space * times <= 64 else [("space",), ("tm",)]
    gathers = []
    for axes in stages:
        count = math.prod(sizes[axis] for axis in axes)
        gathers += [(count, 1, LANES)] + [pltpu.SemaphoreType.DMA((count,))] * 2
    final, table = call(
        functools.partial(third_kernel, plan, stages),
        [(54, rows * planes, LANES), (times, LANES)],
        [gauge, ahead, spread, spread, relay_sems]
        + [(2 * pairs, 8, LANES), (LANES, LANES), (1, LANES)]
        + gathers,
        [scalars, lattice, slab_one, slab_two, spread_one, fold(propagator)],
        2,
        smem=1,
    )
    final = jnp.swapaxes(final.reshape(54, rows, planes, LANES), 1, 2)
    final = final.reshape(links.shape)
    summed = table[:, : 2 * pairs].reshape(times, 2, pairs)
    summed = jnp.swapaxes(summed, 0, 1).reshape(2, 4, 3, SC)
    anchor = jnp.sum(table[:, 2 * pairs : 2 * pairs + 18], axis=0).reshape(2, 3, 3)
    left_re, left_im = summed[0][:, None], summed[1][:, None]
    right_re, right_im = (anchor[i][None, :, :, None] for i in range(2))
    real = jnp.sum(left_re * right_re + left_im * right_im, axis=2)
    imag = jnp.sum(left_im * right_re - left_re * right_im, axis=2)
    wall = jnp.stack([real.reshape(SC * SC), imag.reshape(SC * SC)])
    return final, wall * float(wide * area) ** (-0.5)


def solution(mesh):
    sizes = {axis: mesh.shape[axis] for axis in ("space", "tm")}
    placed = (
        P("tm", None, None, None, None, "space", None),
        P(None, "tm", "space", None),
        P(),
        P(),
        P(),
    )
    return jax.shard_map(
        functools.partial(body, sizes),
        mesh=mesh,
        in_specs=placed,
        out_specs=(P("tm", None, None, None, None, "space", None), P()),
        check_vma=False,
    )
```

profile of v0, /device:TPU:0, one launch (start us, length us, event | category | flops | bytes accessed | tf_op | source)
XLA Modules:
  0.0 79.7 jit_solution(15454777151848267385)
XLA Ops:
  2.7 0.7 stack.30.root_ref.scalar_ref
  3.3 18.2 %shard_map.113.slab_one = f32[24,32,128]{2,1,0:T(8,128)} custom-call(f32[54,64,128]{2,1,0:T(8,128)} %bitcast.37, bf16[384,256]{1,0:T(8,128)(2,1)} %constant.85.clone.right_ref, bf16[64,192]{1,0:T(8,128)(2,1)} %constant.86.clone.left_ref, bf16[384,256]{1,0:T(8,128)(2,1)} %constant.87.clone.back_ref, bf16[64,192]{1,0:T(8,128)(2,1)} %constant.88.clone.turn_ref, ...), custom_call_target="tpu_custom_call" | custom-call | tf_op jit(solution)/shard_map/pallas_call | solution.py:734
  21.5 23.3 %shard_map.114 = (f32[54,2,32,128]{3,2,1,0:T(8,128)}, f32[24,32,128]{2,1,0:T(8,128)}, f32[16,32,128]{2,1,0:T(8,128)}) custom-call(s32[5]{0:T(128)} %stack.30.root_ref.scalar_ref, f32[54,64,128]{2,1,0:T(8,128)} %bitcast.38, f32[24,32,128]{2,1,0:T(8,128)} %shard_map.113.slab_one, bf16[384,256]{1,0:T(8,128)(2,1)} %constant.85.clone.right_ref, ...), custom_call_target="tpu_custom_call" | custom-call | tf_op jit(solution)/shard_map/pallas_call | solution.py:734
  44.9 29.1 %shard_map.115 = (f32[54,64,128]{2,1,0:T(8,128)}, f32[4,128]{1,0:T(4,128)}) custom-call(s32[5]{0:T(128)} %stack.30.root_ref.scalar_ref, f32[54,2,32,128]{3,2,1,0:T(8,128)} %get-tuple-element.7.lattice_ref, f32[24,32,128]{2,1,0:T(8,128)} %shard_map.113.slab_one, f32[24,32,128]{2,1,0:T(8,128)} %get-tuple-element.8.slab_two, ...), custom_call_target="tpu_custom_call" | custom-call | tf_op jit(solution)/shard_map/pallas_call | solution.py:734
  74.0 0.8 slice_reduce_fusion
  74.8 0.1 fusion.1
  74.8 0.1 mul.64
  74.9 0.1 mul.69
  75.0 0.8 reshape.57
  75.8 0.1 mul.62
  75.9 0.1 mul.67
  76.0 0.1 add_reduce_fusion
  76.1 0.1 stack_reshape.6
  76.2 0.1 stack_reshape.7
  76.3 0.6 maximum_multiply_fusion
  76.9 2.9 %copy.33 = f32[1,3,2,3,3,2,4096]{6,5,4,3,2,1,0:T(2,128)} copy(f32[1,3,2,3,3,2,4096]{6,5,4,3,2,1,0:T(2,128)} %bitcast.40) | data formatting | bytes 3538944
  (6 shorter events, 0.0 us)
where the time goes:
time: 80 us; the launch traced here: 79.7 us
  Pallas kernels  70.6 us (88%)
  local copies, waits for them, and re-layouts  4.91 us (6%)
  between operations  2.73 us (3%)
  other arithmetic  1.46 us (2%)
    pallas_call x3, Pallas kernels, call(): pl.pallas_call(kernel, out_shape=[jax.ShapeDtypeStruct(s, jnp.float32) fo...  70.6 us
    unnamed x1, local copies, waits for them, and re-layouts  2.88 us

commit v1 on v0

--- a/solution.py
+++ b/solution.py
@@ -19,6 +19,7 @@
 MESH = pl.DeviceIdType.MESH
 VMEM = pl.BlockSpec(memory_space=pltpu.VMEM)
 SMEM = pl.BlockSpec(memory_space=pltpu.SMEM)
+ANY = pl.BlockSpec(memory_space=pl.ANY)
 LIMIT = 60 * 1024 * 1024
 
 
@@ -290,15 +291,6 @@
         return jnp.where(root == self.me, own, other)
 
 
-def greet(axis, offsets, sizes):
-    barrier = pltpu.get_barrier_semaphore()
-    me = lax.axis_index(axis)
-    for off in offsets:
-        peer = lax.rem(me + off, sizes[axis])
-        pl.semaphore_signal(barrier, inc=1, device_id={axis: peer}, device_id_type=MESH)
-    return len(offsets)
-
-
 class Plan:
     def __init__(self, sizes, planes, rows, basis, moment):
         self.sizes, self.planes, self.rows = sizes, planes, rows
@@ -313,12 +305,6 @@
 
     def fields(self, g):
         return range(g * self.ratio, (g + 1) * self.ratio)
-
-    def exchange_scratch(self):
-        sems = pltpu.SemaphoreType.DMA((self.groups, self.size))
-        return [pltpu.VMEM(self.chunk, jnp.float32)] * 4 + [
-            pltpu.VMEM((len(self.levels), 8, LANES), jnp.float32)
-        ] + [sems] * 4
 
 
 def weigh(plan, yz_ref, weight_ref):
@@ -410,35 +396,6 @@
             send_ref[g, d, p] = out[(d * planes + p) % n]
 
 
-def first_kernel(
-    plan, links_ref, right_ref, left_ref, back_ref, turn_ref, yz_ref, slab_ref,
-    send_one, recv_one, send_two, recv_two, weight_ref, *sems,
-):
-    planes, rows = plan.planes, plan.rows
-    total = greet("space", range(1, plan.size), plan.sizes)
-    one = Swap(plan.size, send_one, recv_one, sems[0], sems[1])
-    two = Swap(plan.size, send_two, recv_two, sems[2], sems[3])
-
-    def u(i, part, a, b, p):
-        return links_ref[i * 18 + at(part, a, b), pl.ds(p, rows, planes), :]
-
-    for g in range(plan.groups):
-        forward(plan, u, g, right_ref[...], left_ref[...], send_one)
-        if g == 0:
-            pl.semaphore_wait(pltpu.get_barrier_semaphore(), total)
-        one.start(g)
-    weigh(plan, yz_ref, weight_ref)
-    for g in range(plan.groups):
-        one.arrive(g)
-        across(plan, g, recv_one, weight_ref, send_two)
-        two.start(g)
-    for g in range(plan.groups):
-        two.arrive(g)
-        backward(plan, g, back_ref[...], turn_ref[...], recv_two, slab_ref)
-    one.drain()
-    two.drain()
-
-
 def gauge_of(slab_ref, planes, gauge_ref):
     rows = gauge_ref.shape[2]
 
@@ -492,75 +449,20 @@
                         put_band(i, r, a, b, p, j, out[a][b][r])
 
 
-def relay_order(chunks, deep):
-    steps = [(k, h) for k in range(chunks) for h in range(1, deep)]
-    return sorted(steps, key=lambda s: 1.4 * (s[0] + s[1]) + 2.1 * s[1])
-
-
-def second_kernel(
-    plan, root_ref, links_ref, slab_one, right_ref, left_ref, back_ref, turn_ref, yz_ref,
-    out_ref, slab_two, spread_ref,
-    send_one, recv_one, send_two, recv_two, weight_ref, sem_a, sem_b, sem_c, sem_d,
-    gauge_ref, ahead_ref, up_ref, down_ref, relay_sems,
-):
-    planes, rows, sizes = plan.planes, plan.rows, plan.sizes
-    total = greet("space", range(1, plan.size), sizes)
-    total += greet("tm", (1, sizes["tm"] - 1), sizes)
-    one = Swap(plan.size, send_one, recv_one, sem_a, sem_b)
-    two = Swap(plan.size, send_two, recv_two, sem_c, sem_d)
-
-    def own(k, j, band=slice(None)):
-        i, p = divmod(j, planes)
-        return slab_one[(k * plan.ratio + i) * (planes + 1) + p, band, :]
-
-    relay = Relay(sizes["tm"], root_ref[0], own, up_ref, down_ref, relay_sems)
-    gauge_of(slab_one, planes, gauge_ref)
-    shift_all(planes, gauge_ref, ahead_ref)
-
-    def get(i, r, a, b, p, j):
-        return links_ref[i * 18 + at(r, a, b), pl.ds(j * 8 * planes + p, 8, planes), :]
-
-    def put(i, r, a, b, p, j, value):
-        out_ref[i * 18 + at(r, a, b), p, pl.ds(pl.multiple_of(j * 8, 8), 8), :] = value
-
-    for p in range(planes):
-        rotate_plane(get, put, p, gauge_ref, ahead_ref)
-
-    def u(i, part, a, b, p):
-        return out_ref[i * 18 + at(part, a, b), p]
-
-    steps = relay_order(plan.groups, relay.deep)
-
-    def advance(count):
-        for _ in range(count):
-            if steps:
-                relay.step(*steps.pop(0))
-
-    pl.semaphore_wait(pltpu.get_barrier_semaphore(), total)
-    for k in range(plan.groups):
-        relay.step(k, 0)
-    for g in range(plan.groups):
-        forward(plan, u, g, right_ref[...], left_ref[...], send_one)
-        one.start(g)
-    weigh(plan, yz_ref, weight_ref)
-    advance(3)
-    for g in range(plan.groups):
-        one.arrive(g)
-        across(plan, g, recv_one, weight_ref, send_two)
-        two.start(g)
-        advance(1)
-    for g in range(plan.groups):
-        advance(1)
-        two.arrive(g)
-        backward(plan, g, back_ref[...], turn_ref[...], recv_two, slab_two)
-    advance(len(steps))
-    for k in range(plan.groups):
-        for j in range(plan.ratio * planes):
-            i, p = divmod(j, planes)
-            spread_ref[(k * plan.ratio + i) * planes + p] = relay.value(k, j, slice(None))
-    one.drain()
-    two.drain()
-    relay.drain()
+class Steps:
+    def __init__(self, relay, start):
+        self.relay, self.start = relay, start
+        chunks = relay.up.shape[0]
+        self.left = sorted(
+            [(k, h) for k in range(chunks) for h in range(1, relay.deep)], key=self.ready
+        )
+
+    def ready(self, step):
+        return self.start + 0.7 * step[0] + 2.8 * step[1]
+
+    def until(self, time, keep=0):
+        while len(self.left) > keep and self.ready(self.left[0]) <= time:
+            self.relay.step(*self.left.pop(0))
 
 
 class Gather:
@@ -605,57 +507,165 @@
             copy.wait()
 
 
-def third_kernel(
-    plan, stages, scalar_ref, lattice_ref, slab_one, slab_two, spread_ref, prop_ref,
+def main_kernel(
+    plan, stages, sink_ref, src_ref, site_ref, links_any, right_any, left_any, back_any,
+    turn_any, yz_any, prop_any,
     out_ref, table_ref,
+    links_ref, right_ref, left_ref, back_ref, turn_ref, yz_ref, prop_ref, load_sems,
+    send_ref, recv_ref, swap_sems, weight_ref, slab_one, slab_two, lattice_ref,
     gauge_ref, ahead_ref, up_ref, down_ref, relay_sems, acc_ref, sum_ref, row_ref, *gathers,
 ):
     planes, rows, sizes = plan.planes, plan.rows, plan.sizes
-    root, present, plane, line, lane = (scalar_ref[i] for i in range(5))
+    space, times = sizes["space"], sizes["tm"]
     stages = [
         Gather(sizes, axes, *gathers[3 * i : 3 * i + 3]) for i, axes in enumerate(stages)
     ]
     total = sum(stage.greet() for stage in stages)
 
-    def own(k, j, band=slice(None)):
-        i, p = divmod(j, planes)
-        return slab_two[(k * plan.ratio + i) * (planes + 1) + p, band, :]
-
-    relay = Relay(sizes["tm"], root, own, up_ref, down_ref, relay_sems)
-    pl.semaphore_wait(pltpu.get_barrier_semaphore(), total)
-    for k in range(plan.groups):
-        relay.step(k, 0)
-    steps = relay_order(plan.groups, relay.deep)
-
-    def advance(count):
-        for _ in range(count):
-            if steps:
-                relay.step(*steps.pop(0))
-
-    gauge_of(slab_two, planes, gauge_ref)
+    pairs_of = [
+        (right_any, right_ref), (left_any, left_ref), (back_any, back_ref),
+        (turn_any, turn_ref), (yz_any, yz_ref), (prop_any, prop_ref),
+    ]
+    early = [
+        pltpu.make_async_copy(
+            links_any.at[pl.ds(i * 18, 18)], links_ref.at[pl.ds(i * 18, 18)], load_sems.at[i]
+        )
+        for i in range(3)
+    ]
+    late = [
+        pltpu.make_async_copy(a, b, load_sems.at[3 + i]) for i, (a, b) in enumerate(pairs_of)
+    ]
+    early += late[:2]
+    late = late[2:]
+    for copy in early + late:
+        copy.start()
+
+    swaps = [
+        Swap(space, send_ref.at[i], recv_ref.at[i], swap_sems.at[2 * i], swap_sems.at[2 * i + 1])
+        for i in range(2 * ITERS)
+    ]
+    root = lax.rem(sink_ref[0], times)
+
+    def owner(slab):
+        def own(k, j, band=slice(None)):
+            g, p = divmod(k, planes)
+            return slab[(g * plan.ratio + j) * (planes + 1) + p, band, :]
+
+        return own
+
+    relays = [
+        Relay(times, root, owner(slab), up_ref.at[i], down_ref.at[i], relay_sems.at[i])
+        for i, slab in enumerate((slab_one, slab_two))
+    ]
+    steps = [Steps(relay, 0.8) for relay in relays]
+
+    def sweep(u, index, before=lambda: None):
+        one, two = swaps[2 * index], swaps[2 * index + 1]
+        slab, relay = (slab_one, slab_two)[index], relays[index]
+        for g in range(plan.groups):
+            forward(plan, u, g, right_ref[...], left_ref[...], one.send)
+            if g == 0:
+                before()
+            one.start(g)
+            if index:
+                steps[0].until(6.5 + 0.3 * g)
+        if index == 0:
+            for copy in late[:3]:
+                copy.wait()
+            weigh(plan, yz_ref, weight_ref)
+        for g in range(plan.groups):
+            if index:
+                steps[0].until(10.6 + 1.05 * g)
+            one.arrive(g)
+            across(plan, g, one.recv, weight_ref, two.send)
+            two.start(g)
+        if index:
+            steps[0].until(1e9)
+        for g in range(plan.groups):
+            two.arrive(g)
+            backward(plan, g, back_ref[...], turn_ref[...], two.recv, slab)
+            for p in range(planes):
+                relay.step(g * planes + p, 0)
+
+    for copy in early:
+        copy.wait()
+
+    def first(i, part, a, b, p):
+        return links_ref[i * 18 + at(part, a, b), pl.ds(p, rows, planes), :]
+
+    sweep(first, 0, lambda: pl.semaphore_wait(pltpu.get_barrier_semaphore(), total))
+    steps[0].until(3.6)
+    gauge_of(slab_one, planes, gauge_ref)
+    steps[0].until(4.3)
     shift_all(planes, gauge_ref, ahead_ref)
 
     def get(i, r, a, b, p, j):
-        return lattice_ref[i * 18 + at(r, a, b), p, pl.ds(pl.multiple_of(j * 8, 8), 8), :]
+        return links_ref[i * 18 + at(r, a, b), pl.ds(j * 8 * planes + p, 8, planes), :]
 
     def put(i, r, a, b, p, j, value):
-        out_ref[i * 18 + at(r, a, b), pl.ds(j * 8 * planes + p, 8, planes), :] = value
+        lattice_ref[i * 18 + at(r, a, b), p, pl.ds(pl.multiple_of(j * 8, 8), 8), :] = value
 
     for p in range(planes):
         rotate_plane(get, put, p, gauge_ref, ahead_ref)
-        advance(2)
+        steps[0].until(5.3 + 0.7 * p)
+
+    sweep(lambda i, part, a, b, p: lattice_ref[i * 18 + at(part, a, b), p], 1)
+
+    time = [3.6]
+
+    def pause(length):
+        time[0] += length
+        steps[1].until(time[0])
+
+    pause(0.0)
+    gauge_of(slab_two, planes, gauge_ref)
+    pause(0.7)
+    shift_all(planes, gauge_ref, ahead_ref)
+    pause(0.4)
+
+    def get_last(i, r, a, b, p, j):
+        return lattice_ref[i * 18 + at(r, a, b), p, pl.ds(pl.multiple_of(j * 8, 8), 8), :]
+
+    def put_last(i, r, a, b, p, j, value):
+        out_ref[i * 18 + at(r, a, b), pl.ds(j * 8 * planes + p, 8, planes), :] = value
+
+    for p in range(planes):
+        rotate_plane(get_last, put_last, p, gauge_ref, ahead_ref)
+        pause(0.7)
+    for p in range(planes):
+
+        @pl.loop(0, rows // 8)
+        def _(j):
+            band = pl.ds(pl.multiple_of(j * 8, 8), 8)
+            one = exponential(
+                [
+                    relays[0].value((f // plan.ratio) * planes + p, f % plan.ratio, band)
+                    for f in range(FIELDS)
+                ]
+            )
+            for a in range(3):
+                for b in range(3):
+                    for part in range(2):
+                        ahead_ref[at(part, a, b), p, band, :] = one[a][b][part]
+
+    pause(0.6)
     acc_ref[...] = jnp.zeros_like(acc_ref)
     sum_ref[...] = jnp.zeros_like(sum_ref)
-    spot = (lax.broadcasted_iota(jnp.int32, (rows, LANES), 0) == line) & (
-        lax.broadcasted_iota(jnp.int32, (rows, LANES), 1) == lane
+    site = site_ref[0]
+    column = lax.rem(site, rows * LANES)
+    plane = lax.div(site, rows * LANES) - lax.axis_index("space") * planes
+    present = lax.rem(src_ref[0], times) == lax.axis_index("tm")
+    present = present & (plane >= 0) & (plane < planes)
+    spot = (lax.broadcasted_iota(jnp.int32, (rows, LANES), 0) == lax.div(column, LANES)) & (
+        lax.broadcasted_iota(jnp.int32, (rows, LANES), 1) == lax.rem(column, LANES)
     )
 
     def pick(ref, f):
-        value = jnp.zeros((1, 1), jnp.float32)
+        value = jnp.zeros((rows, LANES), jnp.float32)
         for p in range(planes):
             here = spot & (plane == p)
-            entry = ref[f * (planes + 1) + p]
-            value = value + jnp.sum(jnp.where(here, entry, 0.0), keepdims=True)
+            value = value + jnp.where(here, ref[f * (planes + 1) + p], 0.0)
+        value = jnp.sum(jnp.sum(value, axis=0, keepdims=True), axis=1, keepdims=True)
         return jnp.broadcast_to(value, (8, LANES))
 
     anchor = matmul3(
@@ -663,28 +673,32 @@
         exponential([pick(slab_one, f) for f in range(FIELDS)]),
     )
     pairs = prop_ref.shape[0] // 2
-    first = lane_of((1, LANES)) == 0
+    first_lane = lane_of((1, LANES)) == 0
     for r in range(2):
         for a in range(3):
             for b in range(3):
                 e = 2 * pairs + at(r, a, b)
                 sum_ref[e : e + 1, :] = jnp.where(
-                    first & (present > 0), anchor[a][b][r][0:1, :], 0.0
+                    first_lane & present, anchor[a][b][r][0:1, :], 0.0
                 )
-    advance(len(steps))
-
+    late[3].wait()
+    pause(1e9) if times == 1 else None
     for p in range(planes):
+        steps[1].until(1e9, keep=planes - 1 - p)
 
         @pl.loop(0, rows // 8)
         def _(j):
             band = pl.ds(pl.multiple_of(j * 8, 8), 8)
-            one = exponential([spread_ref[f * planes + p, band, :] for f in range(FIELDS)])
             two = exponential(
                 [
-                    relay.value(f // plan.ratio, (f % plan.ratio) * planes + p, band)
+                    relays[1].value((f // plan.ratio) * planes + p, f % plan.ratio, band)
                     for f in range(FIELDS)
                 ]
             )
+            one = [
+                [tuple(ahead_ref[at(r, a, b), p, band, :] for r in range(2)) for b in range(3)]
+                for a in range(3)
+            ]
             t = matmul3(two, one)
             for q in range(pairs // 3):
                 s = [
@@ -711,7 +725,6 @@
         precision=EXACT,
         preferred_element_type=jnp.float32,
     )[0:1, :]
-    space, times = sizes["space"], sizes["tm"]
     stages[0].run(row_ref)
     if len(stages) == 1:
         for t in range(times):
@@ -727,22 +740,43 @@
         stages[1].run(row_ref)
         for t in range(times):
             table_ref[t : t + 1, :] = stages[1].target[t]
-    relay.drain()
-
-
-def call(kernel, outs, scratch, args, collective_id, smem=0):
-    return pl.pallas_call(
-        kernel,
-        out_shape=[jax.ShapeDtypeStruct(s, jnp.float32) for s in outs],
-        in_specs=[SMEM] * smem + [VMEM] * (len(args) - smem),
-        out_specs=[VMEM] * len(outs),
-        scratch_shapes=[
-            pltpu.VMEM(s, jnp.float32) if isinstance(s, tuple) else s for s in scratch
-        ],
-        compiler_params=pltpu.CompilerParams(
-            collective_id=collective_id, has_side_effects=True, vmem_limit_bytes=LIMIT
-        ),
-    )(*args)
+    for swap in swaps:
+        swap.drain()
+    for relay in relays:
+        relay.drain()
+
+
+def close_kernel(pairs, scale, table_ref, wall_ref, flat_ref):
+    times = table_ref.shape[0]
+    flat_ref[...] = jnp.zeros_like(flat_ref)
+    for t in range(times):
+        for r in range(2):
+            flat_ref[r : r + 1, t * pairs : (t + 1) * pairs] = table_ref[
+                t : t + 1, r * pairs : (r + 1) * pairs
+            ]
+    length = flat_ref.shape[1]
+    entry = jnp.sum(table_ref[...], axis=0, keepdims=True)
+    lanes = lax.broadcasted_iota(jnp.int32, (1, length), 1)
+    colour = lax.rem(lax.div(lanes, SC), 3)
+    re, im = flat_ref[0:1, :], flat_ref[1:2, :]
+    real = imag = jnp.zeros((1, length), jnp.float32)
+    for gap in range(-2, 3):
+        xr = pltpu.roll(re, (gap * SC) % length, 1) if gap else re
+        xi = pltpu.roll(im, (gap * SC) % length, 1) if gap else im
+        for b in range(3):
+            c = b - gap
+            if 0 <= c < 3:
+                ar, ai = (
+                    jnp.broadcast_to(
+                        entry[:, 2 * pairs + at(r, b, c) : 2 * pairs + at(r, b, c) + 1],
+                        (1, length),
+                    )
+                    for r in range(2)
+                )
+                real = real + jnp.where(colour == b, xr * ar + xi * ai, 0.0)
+                imag = imag + jnp.where(colour == b, xi * ar - xr * ai, 0.0)
+    wall_ref[0:1, :] = real[:, : SC * SC] * scale
+    wall_ref[1:2, :] = imag[:, : SC * SC] * scale
 
 
 def body(sizes, links, propagator, sink_time, src_time, src_site):
@@ -766,73 +800,50 @@
         x = x.reshape(lead + (planes, rows, LANES))
         return jnp.swapaxes(x, -3, -2).reshape((-1, rows * planes, LANES))
 
-    linked = fold(links[0])
-    field = (FIELDS * planes, rows, LANES)
-    gauge = (18, planes + 1, rows, LANES)
-    ahead = (36, planes, rows, LANES)
-    split = (54, planes, rows, LANES)
-    spread = (plan.groups, plan.ratio * planes, rows, LANES)
-    relay_sems = pltpu.SemaphoreType.DMA((4, plan.groups))
-
-    site = src_site[0]
-    space_index = lax.axis_index("space")
-    time_index = lax.axis_index("tm")
-    plane = site // area - space_index * planes
-    column = site % area
-    present = (src_time[0] % times == time_index) & (plane >= 0) & (plane < planes)
-    scalars = jnp.stack(
-        [
-            sink_time[0] % times,
-            present.astype(jnp.int32),
-            plane,
-            column // LANES,
-            column % LANES,
-        ]
-    )
-
-    (slab_one,) = call(
-        functools.partial(first_kernel, plan),
-        [plan.slab],
-        plan.exchange_scratch(),
-        [linked, right, left, back, turn, yz],
-        0,
-    )
-    lattice, slab_two, spread_one = call(
-        functools.partial(second_kernel, plan),
-        [split, plan.slab, field],
-        plan.exchange_scratch() + [gauge, ahead, spread, spread, relay_sems],
-        [scalars, linked, slab_one, right, left, back, turn, yz],
-        1,
-        smem=1,
-    )
+    linked, source = fold(links[0]), fold(propagator)
     pairs = propagator.shape[1]
     assert 2 * pairs + 18 <= LANES
     stages = [("space", "tm")] if space * times <= 64 else [("space",), ("tm",)]
+    vmem = lambda *shape: pltpu.VMEM(shape, jnp.float32)
+    sems = pltpu.SemaphoreType.DMA
+    chunks = plan.groups * planes
     gathers = []
     for axes in stages:
         count = math.prod(sizes[axis] for axis in axes)
-        gathers += [(count, 1, LANES)] + [pltpu.SemaphoreType.DMA((count,))] * 2
-    final, table = call(
-        functools.partial(third_kernel, plan, stages),
-        [(54, rows * planes, LANES), (times, LANES)],
-        [gauge, ahead, spread, spread, relay_sems]
-        + [(2 * pairs, 8, LANES), (LANES, LANES), (1, LANES)]
-        + gathers,
-        [scalars, lattice, slab_one, slab_two, spread_one, fold(propagator)],
-        2,
-        smem=1,
-    )
+        gathers += [vmem(count, 1, LANES), sems((count,)), sems((count,))]
+    tables = [right, left, back, turn]
+    scratch = [vmem(*linked.shape)]
+    scratch += [pltpu.VMEM(m.shape, jnp.bfloat16) for m in tables]
+    scratch += [vmem(*yz.shape), vmem(*source.shape), sems((9,))]
+    scratch += [vmem(2 * ITERS, *plan.chunk)] * 2
+    scratch += [sems((4 * ITERS, plan.groups, space)), vmem(len(plan.levels), 8, LANES)]
+    scratch += [vmem(*plan.slab)] * 2 + [vmem(54, planes, rows, LANES)]
+    scratch += [vmem(18, planes + 1, rows, LANES), vmem(36, planes, rows, LANES)]
+    scratch += [vmem(ITERS, chunks, plan.ratio, rows, LANES)] * 2
+    scratch += [sems((ITERS, 4, chunks))]
+    scratch += [vmem(2 * pairs, 8, LANES), vmem(LANES, LANES), vmem(1, LANES)]
+    final, table = pl.pallas_call(
+        functools.partial(main_kernel, plan, stages),
+        out_shape=[
+            pltpu.VMEM(linked.shape, jnp.float32),
+            pltpu.VMEM((times, LANES), jnp.float32),
+        ],
+        in_specs=[SMEM] * 3 + [ANY] * 7,
+        out_specs=[VMEM] * 2,
+        scratch_shapes=scratch + gathers,
+        compiler_params=pltpu.CompilerParams(
+            collective_id=0, has_side_effects=True, vmem_limit_bytes=LIMIT
+        ),
+    )(sink_time, src_time, src_site, linked, *tables, yz, source)
+    wall = pl.pallas_call(
+        functools.partial(close_kernel, pairs, float(wide * area) ** (-0.5)),
+        out_shape=jax.ShapeDtypeStruct((2, SC * SC), jnp.float32),
+        in_specs=[VMEM],
+        out_specs=VMEM,
+        scratch_shapes=[vmem(8, 2 * LANES)],
+    )(pltpu.with_memory_space_constraint(table, pltpu.VMEM))
     final = jnp.swapaxes(final.reshape(54, rows, planes, LANES), 1, 2)
-    final = final.reshape(links.shape)
-    summed = table[:, : 2 * pairs].reshape(times, 2, pairs)
-    summed = jnp.swapaxes(summed, 0, 1).reshape(2, 4, 3, SC)
-    anchor = jnp.sum(table[:, 2 * pairs : 2 * pairs + 18], axis=0).reshape(2, 3, 3)
-    left_re, left_im = summed[0][:, None], summed[1][:, None]
-    right_re, right_im = (anchor[i][None, :, :, None] for i in range(2))
-    real = jnp.sum(left_re * right_re + left_im * right_im, axis=2)
-    imag = jnp.sum(left_im * right_re - left_re * right_im, axis=2)
-    wall = jnp.stack([real.reshape(SC * SC), imag.reshape(SC * SC)])
-    return final, wall * float(wide * area) ** (-0.5)
+    return final.reshape(links.shape), wall
 
 
 def solution(mesh):

time: 80 us -> 59 us (0.74)
  Pallas kernels: 70.6 us -> 55.1 us
  local copies, waits for them, and re-layouts: 4.91 us -> 1.21 us
  other arithmetic: 1.46 us -> 0 us
    pallas_call x3 -> x2, Pallas kernels: 70.6 us -> 55.1 us  [the longest x1 54.3 us: body(): pl.pallas_call(functools.partial(main_kernel, plan, stages), out_shape=[p...]
    unnamed x1, local copies, waits for them, and re-layouts: 2.88 us -> 1.21 us
    reduce_sum x2 -> x0, other arithmetic: 0.87 us -> none  [the longest x1 0.77 us: body(): jnp.sum(table[:, 2 * pairs:2 * pairs + 18], axis=0).reshape(2, 3, 3)]
    another operation x3 -> x0, local copies, waits for them, and re-layouts: 0.83 us -> none  [the longest x1 0.67 us: body(): jnp.stack([sink_time[0] % times, present.astype(jnp.int32), plane, column...]
where the time goes in v1:
time: 59 us; the launch traced here: 58.8 us
  Pallas kernels  55.1 us (93%)
  between operations  2.58 us (4%)
  local copies, waits for them, and re-layouts  1.21 us (2%)
    pallas_call x1, Pallas kernels, body(): pl.pallas_call(functools.partial(main_kernel, plan, stages), out_shape=[p...  54.3 us
    unnamed x1, local copies, waits for them, and re-layouts  1.21 us

profile of v1, /device:TPU:0, one launch (start us, length us, event | category | flops | bytes accessed | tf_op | source)
XLA Modules:
  0.0 58.8 jit_solution(7297941586690162231)
XLA Ops:
  2.6 54.3 %shard_map.113 = (f32[54,64,128]{2,1,0:T(8,128)S(1)}, f32[4,128]{1,0:T(4,128)S(1)}) custom-call(s32[1]{0:T(128)S(6)} %copy.17.sink_ref, s32[1]{0:T(128)S(6)} %copy.18.src_ref, s32[1]{0:T(128)S(6)} %copy.19.site_ref, f32[54,64,128]{2,1,0:T(8,128)} %bitcast.17, bf16[384,256]{1,0:T(8,128)(2,1)} %constant.10.clone.right_any, ...), custom_call_target="tpu_custom_call" | custom-call | tf_op jit(solution)/shard_map/pallas_call | solution.py:825
  56.9 1.2 %copy.16 = f32[1,3,2,3,3,2,4096]{6,5,4,3,2,1,0:T(2,128)} copy(f32[1,3,2,3,3,2,4096]{6,5,4,3,2,1,0:T(2,128)S(1)} %bitcast.15) | data formatting | bytes 3538944
  58.1 0.8 %shard_map.114 = f32[2,144]{1,0:T(2,128)} custom-call(f32[4,128]{1,0:T(4,128)S(1)} %get-tuple-element.5.table_ref), custom_call_target="tpu_custom_call" | custom-call | tf_op jit(solution)/shard_map/pallas_call | solution.py:838

commit v2 on v1

--- a/solution.py
+++ b/solution.py
@@ -15,11 +15,11 @@
 PEAK = 12.0
 LANES = 128
 FIELDS = 8
+PIECES = 6
 EXACT = lax.Precision.HIGHEST
 MESH = pl.DeviceIdType.MESH
 VMEM = pl.BlockSpec(memory_space=pltpu.VMEM)
-SMEM = pl.BlockSpec(memory_space=pltpu.SMEM)
-ANY = pl.BlockSpec(memory_space=pl.ANY)
+HBM = pl.BlockSpec(memory_space=pltpu.HBM)
 LIMIT = 60 * 1024 * 1024
 
 
@@ -262,7 +262,7 @@
                         buffer[k, j] = self.own(k, j)
                 else:
                     self.hop(k, rise).wait_recv()
-                    mine = jnp.broadcast_to(self.root, buffer.shape[2:]) == self.me
+                    mine = jnp.broadcast_to(lax.rem(self.root[0], self.size), buffer.shape[2:]) == self.me
                     for j in range(parts):
                         buffer[k, j] = jnp.where(mine, self.own(k, j), buffer[k, j])
                 if not last:
@@ -286,9 +286,32 @@
 
     def value(self, k, j, band):
         own = self.own(k, j, band)
-        root = jnp.broadcast_to(self.root, own.shape)
+        root = jnp.broadcast_to(lax.rem(self.root[0], self.size), own.shape)
         other = jnp.where(root < self.me, self.up[k, j, band, :], self.down[k, j, band, :])
         return jnp.where(root == self.me, own, other)
+
+
+def greet(sizes):
+    barrier = pltpu.get_barrier_semaphore()
+    me, time = lax.axis_index("space"), lax.axis_index("tm")
+    size, times = sizes["space"], sizes["tm"]
+
+    def signal(peer):
+        pl.semaphore_signal(barrier, inc=1, device_id=peer, device_id_type=MESH)
+
+    for off in range(1, size):
+        signal({"space": lax.rem(me + off, size)})
+    above, below = time < times - 1, time > 0
+
+    @pl.when(above)
+    def _():
+        signal({"tm": lax.rem(time + 1, times)})
+
+    @pl.when(below)
+    def _():
+        signal({"tm": lax.rem(time + times - 1, times)})
+
+    return size - 1 + above.astype(jnp.int32) + below.astype(jnp.int32)
 
 
 class Plan:
@@ -482,12 +505,6 @@
                 rest //= size
             self.peers.append((flat, peer))
 
-    def greet(self):
-        barrier = pltpu.get_barrier_semaphore()
-        for _, peer in self.peers:
-            pl.semaphore_signal(barrier, inc=1, device_id=peer, device_id_type=MESH)
-        return len(self.peers)
-
     def run(self, source):
         copies = []
         for flat, peer in self.peers:
@@ -508,9 +525,10 @@
 
 
 def main_kernel(
-    plan, stages, sink_ref, src_ref, site_ref, links_any, right_any, left_any, back_any,
+    plan, stages, sink_any, src_any, site_any, links_any, right_any, left_any, back_any,
     turn_any, yz_any, prop_any,
     out_ref, table_ref,
+    sink_ref, src_ref, site_ref,
     links_ref, right_ref, left_ref, back_ref, turn_ref, yz_ref, prop_ref, load_sems,
     send_ref, recv_ref, swap_sems, weight_ref, slab_one, slab_two, lattice_ref,
     gauge_ref, ahead_ref, up_ref, down_ref, relay_sems, acc_ref, sum_ref, row_ref, *gathers,
@@ -520,11 +538,12 @@
     stages = [
         Gather(sizes, axes, *gathers[3 * i : 3 * i + 3]) for i, axes in enumerate(stages)
     ]
-    total = sum(stage.greet() for stage in stages)
+    total = greet(sizes)
 
     pairs_of = [
         (right_any, right_ref), (left_any, left_ref), (back_any, back_ref),
-        (turn_any, turn_ref), (yz_any, yz_ref), (prop_any, prop_ref),
+        (turn_any, turn_ref), (yz_any, yz_ref), (sink_any, sink_ref), (src_any, src_ref),
+        (site_any, site_ref), (prop_any, prop_ref),
     ]
     early = [
         pltpu.make_async_copy(
@@ -544,7 +563,6 @@
         Swap(space, send_ref.at[i], recv_ref.at[i], swap_sems.at[2 * i], swap_sems.at[2 * i + 1])
         for i in range(2 * ITERS)
     ]
-    root = lax.rem(sink_ref[0], times)
 
     def owner(slab):
         def own(k, j, band=slice(None)):
@@ -554,7 +572,7 @@
         return own
 
     relays = [
-        Relay(times, root, owner(slab), up_ref.at[i], down_ref.at[i], relay_sems.at[i])
+        Relay(times, sink_ref, owner(slab), up_ref.at[i], down_ref.at[i], relay_sems.at[i])
         for i, slab in enumerate((slab_one, slab_two))
     ]
     steps = [Steps(relay, 0.8) for relay in relays]
@@ -570,7 +588,7 @@
             if index:
                 steps[0].until(6.5 + 0.3 * g)
         if index == 0:
-            for copy in late[:3]:
+            for copy in late[:-1]:
                 copy.wait()
             weigh(plan, yz_ref, weight_ref)
         for g in range(plan.groups):
@@ -649,6 +667,8 @@
                         ahead_ref[at(part, a, b), p, band, :] = one[a][b][part]
 
     pause(0.6)
+    for swap in swaps:
+        swap.drain()
     acc_ref[...] = jnp.zeros_like(acc_ref)
     sum_ref[...] = jnp.zeros_like(sum_ref)
     site = site_ref[0]
@@ -681,7 +701,7 @@
                 sum_ref[e : e + 1, :] = jnp.where(
                     first_lane & present, anchor[a][b][r][0:1, :], 0.0
                 )
-    late[3].wait()
+    late[-1].wait()
     pause(1e9) if times == 1 else None
     for p in range(planes):
         steps[1].until(1e9, keep=planes - 1 - p)
@@ -740,13 +760,20 @@
         stages[1].run(row_ref)
         for t in range(times):
             table_ref[t : t + 1, :] = stages[1].target[t]
-    for swap in swaps:
-        swap.drain()
     for relay in relays:
         relay.drain()
 
 
-def close_kernel(pairs, scale, table_ref, wall_ref, flat_ref):
+def close_kernel(pairs, scale, final_ref, table_ref, out_ref, wall_ref, flat_ref, sem):
+    share = final_ref.shape[0] // PIECES
+    copies = [
+        pltpu.make_async_copy(
+            final_ref.at[pl.ds(i * share, share)], out_ref.at[pl.ds(i * share, share)], sem.at[i]
+        )
+        for i in range(PIECES)
+    ]
+    for copy in copies:
+        copy.start()
     times = table_ref.shape[0]
     flat_ref[...] = jnp.zeros_like(flat_ref)
     for t in range(times):
@@ -777,6 +804,8 @@
                 imag = imag + jnp.where(colour == b, xi * ar - xr * ai, 0.0)
     wall_ref[0:1, :] = real[:, : SC * SC] * scale
     wall_ref[1:2, :] = imag[:, : SC * SC] * scale
+    for copy in copies:
+        copy.wait()
 
 
 def body(sizes, links, propagator, sink_time, src_time, src_site):
@@ -812,9 +841,9 @@
         count = math.prod(sizes[axis] for axis in axes)
         gathers += [vmem(count, 1, LANES), sems((count,)), sems((count,))]
     tables = [right, left, back, turn]
-    scratch = [vmem(*linked.shape)]
+    scratch = [pltpu.SMEM((1,), jnp.int32)] * 3 + [vmem(*linked.shape)]
     scratch += [pltpu.VMEM(m.shape, jnp.bfloat16) for m in tables]
-    scratch += [vmem(*yz.shape), vmem(*source.shape), sems((9,))]
+    scratch += [vmem(*yz.shape), vmem(*source.shape), sems((12,))]
     scratch += [vmem(2 * ITERS, *plan.chunk)] * 2
     scratch += [sems((4 * ITERS, plan.groups, space)), vmem(len(plan.levels), 8, LANES)]
     scratch += [vmem(*plan.slab)] * 2 + [vmem(54, planes, rows, LANES)]
@@ -828,20 +857,23 @@
             pltpu.VMEM(linked.shape, jnp.float32),
             pltpu.VMEM((times, LANES), jnp.float32),
         ],
-        in_specs=[SMEM] * 3 + [ANY] * 7,
+        in_specs=[HBM] * 10,
         out_specs=[VMEM] * 2,
         scratch_shapes=scratch + gathers,
         compiler_params=pltpu.CompilerParams(
             collective_id=0, has_side_effects=True, vmem_limit_bytes=LIMIT
         ),
     )(sink_time, src_time, src_site, linked, *tables, yz, source)
-    wall = pl.pallas_call(
+    final, wall = pl.pallas_call(
         functools.partial(close_kernel, pairs, float(wide * area) ** (-0.5)),
-        out_shape=jax.ShapeDtypeStruct((2, SC * SC), jnp.float32),
-        in_specs=[VMEM],
-        out_specs=VMEM,
-        scratch_shapes=[vmem(8, 2 * LANES)],
-    )(pltpu.with_memory_space_constraint(table, pltpu.VMEM))
+        out_shape=[
+            jax.ShapeDtypeStruct(linked.shape, jnp.float32),
+            jax.ShapeDtypeStruct((2, SC * SC), jnp.float32),
+        ],
+        in_specs=[VMEM] * 2,
+        out_specs=[HBM, VMEM],
+        scratch_shapes=[vmem(8, 2 * LANES), sems((PIECES,))],
+    )(*(pltpu.with_memory_space_constraint(x, pltpu.VMEM) for x in (final, table)))
     final = jnp.swapaxes(final.reshape(54, rows, planes, LANES), 1, 2)
     return final.reshape(links.shape), wall
 

time: 59 us -> 57.9 us (0.981)
  local copies, waits for them, and re-layouts: 1.21 us -> 0 us
    unnamed x1 -> x0, local copies, waits for them, and re-layouts: 1.21 us -> none
    pallas_call x1, Pallas kernels: 0.76 us -> 1.83 us  [body(): pl.pallas_call(functools.partial(close_kernel, pairs, float(wide * area)...]
    pallas_call x1, Pallas kernels: 54.3 us -> 53.4 us  [body(): pl.pallas_call(functools.partial(main_kernel, plan, stages), out_shape=[p...]
where the time goes in v2:
time: 57.9 us; the launch traced here: 57.8 us
  Pallas kernels  55.2 us (95%)
  between operations  2.58 us (4%)
    pallas_call x1, Pallas kernels, body(): pl.pallas_call(functools.partial(main_kernel, plan, stages), out_shape=[p...  53.4 us
    pallas_call x1, Pallas kernels, body(): pl.pallas_call(functools.partial(close_kernel, pairs, float(wide * area)...  1.83 us

profile of v2, /device:TPU:0, one launch (start us, length us, event | category | flops | bytes accessed | tf_op | source)
XLA Modules:
  0.0 57.8 jit_solution(18163478116334793556)
XLA Ops:
  2.6 53.4 %shard_map.113 = (f32[54,64,128]{2,1,0:T(8,128)S(1)}, f32[4,128]{1,0:T(4,128)S(1)}) custom-call(s32[1]{0:T(128)S(6)} %copy.15.sink_any, s32[1]{0:T(128)S(6)} %copy.16.src_any, s32[1]{0:T(128)S(6)} %copy.17.site_any, f32[54,64,128]{2,1,0:T(8,128)} %bitcast.16, bf16[384,256]{1,0:T(8,128)(2,1)} %constant.10.clone.right_any, ...), custom_call_target="tpu_custom_call" | custom-call | tf_op jit(solution)/shard_map/pallas_call | solution.py:854
  55.9 1.8 %shard_map.114 = (f32[54,64,128]{2,1,0:T(8,128)}, f32[2,144]{1,0:T(2,128)}) custom-call(f32[54,64,128]{2,1,0:T(8,128)S(1)} %get-tuple-element.6.final_ref, f32[4,128]{1,0:T(4,128)S(1)} %get-tuple-element.7.table_ref), custom_call_target="tpu_custom_call" | custom-call | tf_op jit(solution)/shard_map/pallas_call | solution.py:867

commit v3 on v2

--- a/solution.py
+++ b/solution.py
@@ -323,7 +323,8 @@
         self.groups = FIELDS // self.ratio
         assert self.ratio * rows == 8 * self.size and self.groups * self.ratio == FIELDS
         self.levels = sorted(set(np.round(moment, 9)))
-        self.chunk = (self.groups, self.size, planes + 1, 8, LANES)
+        assert planes == 2
+        self.chunk = (self.groups, self.size, planes, 8, LANES)
         self.slab = (FIELDS * (planes + 1), rows, LANES)
 
     def fields(self, g):
@@ -333,16 +334,23 @@
 def weigh(plan, yz_ref, weight_ref):
     block = lax.div(lax.axis_index("space"), plan.ratio)
     yz = yz_ref[pl.ds(pl.multiple_of(block * 8, 8), 8), :]
+    above = PEAK * (yz + 2.0)
+    base = yz * (yz + 4.0)
     for index, level in enumerate(plan.levels):
-        p2 = yz + float(level)
+        p2 = base + float(level)
         if level == 0.0:
-            weight = jnp.where(p2 > 0.0, PEAK / jnp.where(p2 > 0.0, p2, 1.0), 0.0)
+            weight = jnp.where(p2 > 0.0, above / jnp.where(p2 > 0.0, p2, 1.0), 0.0)
         else:
-            weight = PEAK / p2
+            weight = above / p2
         weight_ref[index] = weight
 
 
-def forward(plan, u, g, right, left, send_ref):
+def origin(shape, block=0):
+    row = lax.broadcasted_iota(jnp.int32, shape, 0) + block
+    return (row == 0) & (lane_of(shape) == 0)
+
+
+def forward(plan, u, g, right, left, ratio_ref, odd_ref, send_ref):
     planes = plan.planes
     slabs = []
     for f in plan.fields(g):
@@ -356,37 +364,45 @@
             before = x
         slabs.append(before)
     done = plane_transform(slabs, right, left)
-    for index, slab in enumerate(done):
-        i, p = divmod(index, planes + 1)
+    ratio = ratio_ref[...]
+    for i, f in enumerate(plan.fields(g)):
+        even, odd, edge = done[3 * i : 3 * i + 3]
+        odd_ref[f] = odd
+        share = ratio * odd
+        own, other = even + share, jnp.where(origin(odd.shape), odd, edge + share)
         for block in range(plan.rows // 8):
-            send_ref[g, block * plan.ratio + i, p] = slab[block * 8 : block * 8 + 8, :]
-
-
-def backward(plan, g, right, left, recv_ref, slab_ref):
+            band = slice(block * 8, block * 8 + 8)
+            send_ref[g, block * plan.ratio + i, 0] = own[band, :]
+            send_ref[g, block * plan.ratio + i, 1] = other[band, :]
+
+
+def backward(plan, g, right, left, ratio_ref, odd_ref, recv_ref, slab_ref):
     slabs = []
-    for i in range(plan.ratio):
-        for p in range(plan.planes + 1):
-            slabs.append(
-                jnp.concatenate(
-                    [recv_ref[g, b * plan.ratio + i, p] for b in range(plan.rows // 8)],
-                    axis=0,
-                )
+    ratio = ratio_ref[...]
+    for i, f in enumerate(plan.fields(g)):
+        here, ahead = (
+            jnp.concatenate(
+                [recv_ref[g, b * plan.ratio + i, p] for b in range(plan.rows // 8)], axis=0
             )
+            for p in range(2)
+        )
+        slabs += [here, (PEAK * odd_ref[f] + here + ahead) * ratio, ahead]
     base = g * plan.ratio * (plan.planes + 1)
     for index, slab in enumerate(plane_transform(slabs, right, left)):
         slab_ref[base + index] = slab
 
 
 def across(plan, g, recv_ref, weight_ref, send_ref):
-    planes, count, basis = plan.planes, plan.size, plan.basis
-    n = basis.shape[0]
-    v = []
-    for s in range(count):
-        for p in range(planes):
-            value = recv_ref[g, s, p]
-            if p == 0:
-                value = value + recv_ref[g, (s - 1) % count, planes]
-            v.append(value)
+    n, basis = plan.size, plan.basis
+    zero = origin((8, LANES), lax.div(lax.axis_index("space"), plan.ratio))
+    own = [recv_ref[g, s, 0] for s in range(n)]
+    other = [recv_ref[g, s, 1] for s in range(n)]
+    shift = other[0]
+    for s in range(1, n):
+        shift = shift + other[s]
+    shift = jnp.where(zero, shift * (-0.25 * PEAK / n), 0.0)
+    other = [jnp.where(zero, -own[s], other[s]) for s in range(n)]
+    v = [own[s] + other[(s - 1) % n] for s in range(n)]
     half = range(1, (n + 1) // 2)
     even = {0: v[0]}
     odd = {}
@@ -414,9 +430,10 @@
     for x in half:
         out[x] = back_even[x] + back_odd[x]
         out[n - x] = back_even[x] - back_odd[x]
-    for d in range(count):
-        for p in range(planes + 1):
-            send_ref[g, d, p] = out[(d * planes + p) % n]
+    out = [value + shift for value in out]
+    for d in range(n):
+        send_ref[g, d, 0] = out[d]
+        send_ref[g, d, 1] = out[(d + 1) % n]
 
 
 def gauge_of(slab_ref, planes, gauge_ref):
@@ -473,15 +490,15 @@
 
 
 class Steps:
-    def __init__(self, relay, start):
-        self.relay, self.start = relay, start
+    def __init__(self, relay, start, gap, hop):
+        self.relay, self.start, self.gap, self.hop = relay, start, gap, hop
         chunks = relay.up.shape[0]
         self.left = sorted(
             [(k, h) for k in range(chunks) for h in range(1, relay.deep)], key=self.ready
         )
 
     def ready(self, step):
-        return self.start + 0.7 * step[0] + 2.8 * step[1]
+        return self.start + self.gap * step[0] + self.hop * step[1]
 
     def until(self, time, keep=0):
         while len(self.left) > keep and self.ready(self.left[0]) <= time:
@@ -530,8 +547,8 @@
     out_ref, table_ref,
     sink_ref, src_ref, site_ref,
     links_ref, right_ref, left_ref, back_ref, turn_ref, yz_ref, prop_ref, load_sems,
-    send_ref, recv_ref, swap_sems, weight_ref, slab_one, slab_two, lattice_ref,
-    gauge_ref, ahead_ref, up_ref, down_ref, relay_sems, acc_ref, sum_ref, row_ref, *gathers,
+    send_ref, recv_ref, swap_sems, weight_ref, ratio_ref, odd_ref, slab_one, slab_two, lattice_ref,
+    gauge_ref, ahead_ref, up_one, down_one, sems_one, up_two, down_two, sems_two, acc_ref, sum_ref, row_ref, *gathers,
 ):
     planes, rows, sizes = plan.planes, plan.rows, plan.sizes
     space, times = sizes["space"], sizes["tm"]
@@ -541,8 +558,8 @@
     total = greet(sizes)
 
     pairs_of = [
-        (right_any, right_ref), (left_any, left_ref), (back_any, back_ref),
-        (turn_any, turn_ref), (yz_any, yz_ref), (sink_any, sink_ref), (src_any, src_ref),
+        (right_any, right_ref), (left_any, left_ref), (yz_any, yz_ref),
+        (back_any, back_ref), (turn_any, turn_ref), (sink_any, sink_ref), (src_any, src_ref),
         (site_any, site_ref), (prop_any, prop_ref),
     ]
     early = [
@@ -554,8 +571,8 @@
     late = [
         pltpu.make_async_copy(a, b, load_sems.at[3 + i]) for i, (a, b) in enumerate(pairs_of)
     ]
-    early += late[:2]
-    late = late[2:]
+    early += late[:3]
+    late = late[3:]
     for copy in early + late:
         copy.start()
 
@@ -564,57 +581,62 @@
         for i in range(2 * ITERS)
     ]
 
-    def owner(slab):
-        def own(k, j, band=slice(None)):
-            g, p = divmod(k, planes)
-            return slab[(g * plan.ratio + j) * (planes + 1) + p, band, :]
-
-        return own
+    def own_one(k, j, band=slice(None)):
+        g, p = divmod(k, planes)
+        return slab_one[(g * plan.ratio + j) * (planes + 1) + p, band, :]
+
+    def own_two(k, j, band=slice(None)):
+        f, p = divmod(k, planes)
+        return slab_two[f * (planes + 1) + p, band, :]
 
     relays = [
-        Relay(times, sink_ref, owner(slab), up_ref.at[i], down_ref.at[i], relay_sems.at[i])
-        for i, slab in enumerate((slab_one, slab_two))
+        Relay(times, sink_ref, own_one, up_one, down_one, sems_one),
+        Relay(times, sink_ref, own_two, up_two, down_two, sems_two),
     ]
-    steps = [Steps(relay, 0.8) for relay in relays]
+    steps = [Steps(relays[0], 1.5, 0.7, 3.5), Steps(relays[1], 0.6, 0.35, 3.0)]
 
     def sweep(u, index, before=lambda: None):
         one, two = swaps[2 * index], swaps[2 * index + 1]
         slab, relay = (slab_one, slab_two)[index], relays[index]
         for g in range(plan.groups):
-            forward(plan, u, g, right_ref[...], left_ref[...], one.send)
+            forward(plan, u, g, right_ref[...], left_ref[...], ratio_ref, odd_ref, one.send)
             if g == 0:
                 before()
             one.start(g)
             if index:
-                steps[0].until(6.5 + 0.3 * g)
+                steps[0].until(5.5 + 0.3 * g)
         if index == 0:
             for copy in late[:-1]:
                 copy.wait()
             weigh(plan, yz_ref, weight_ref)
         for g in range(plan.groups):
             if index:
-                steps[0].until(10.6 + 1.05 * g)
+                steps[0].until(9.3 + 0.7 * g)
             one.arrive(g)
             across(plan, g, one.recv, weight_ref, two.send)
             two.start(g)
-        if index:
-            steps[0].until(1e9)
         for g in range(plan.groups):
+            if index:
+                steps[0].until(13.0 + 0.7 * g)
             two.arrive(g)
-            backward(plan, g, back_ref[...], turn_ref[...], two.recv, slab)
-            for p in range(planes):
-                relay.step(g * planes + p, 0)
+            backward(
+                plan, g, back_ref[...], turn_ref[...], ratio_ref, odd_ref, two.recv, slab
+            )
+            count = planes * (plan.ratio if index else 1)
+            for k in range(count):
+                relay.step(g * count + k, 0)
 
     for copy in early:
         copy.wait()
+    ratio_ref[...] = 1.0 / (yz_ref[...] + 2.0)
 
     def first(i, part, a, b, p):
         return links_ref[i * 18 + at(part, a, b), pl.ds(p, rows, planes), :]
 
     sweep(first, 0, lambda: pl.semaphore_wait(pltpu.get_barrier_semaphore(), total))
-    steps[0].until(3.6)
+    steps[0].until(2.5)
     gauge_of(slab_one, planes, gauge_ref)
-    steps[0].until(4.3)
+    steps[0].until(3.2)
     shift_all(planes, gauge_ref, ahead_ref)
 
     def get(i, r, a, b, p, j):
@@ -625,11 +647,11 @@
 
     for p in range(planes):
         rotate_plane(get, put, p, gauge_ref, ahead_ref)
-        steps[0].until(5.3 + 0.7 * p)
+        steps[0].until(4.3 + 0.7 * p)
 
     sweep(lambda i, part, a, b, p: lattice_ref[i * 18 + at(part, a, b), p], 1)
 
-    time = [3.6]
+    time = [2.5]
 
     def pause(length):
         time[0] += length
@@ -650,6 +672,7 @@
     for p in range(planes):
         rotate_plane(get_last, put_last, p, gauge_ref, ahead_ref)
         pause(0.7)
+    steps[0].until(1e9)
     for p in range(planes):
 
         @pl.loop(0, rows // 8)
@@ -711,7 +734,7 @@
             band = pl.ds(pl.multiple_of(j * 8, 8), 8)
             two = exponential(
                 [
-                    relays[1].value((f // plan.ratio) * planes + p, f % plan.ratio, band)
+                    relays[1].value(f * planes + p, 0, band)
                     for f in range(FIELDS)
                 ]
             )
@@ -738,11 +761,13 @@
 
     for e in range(2 * pairs):
         sum_ref[e : e + 1, :] = jnp.sum(acc_ref[e], axis=0, keepdims=True)
+    total = sum_ref[...]
+    high = total.astype(jnp.bfloat16)
+    low = (total - high.astype(jnp.float32)).astype(jnp.bfloat16)
     row_ref[...] = lax.dot_general(
-        jnp.ones((8, LANES), jnp.float32),
-        sum_ref[...],
+        jnp.ones((16, 2 * LANES), jnp.bfloat16),
+        jnp.concatenate([high, low], axis=1),
         (((1,), (1,)), ((), ())),
-        precision=EXACT,
         preferred_element_type=jnp.float32,
     )[0:1, :]
     stages[0].run(row_ref)
@@ -819,7 +844,7 @@
     basis, moment = real_basis(side)
     right, left = plane_matrices(basis)
     back, turn = plane_matrices(basis.T)
-    x_basis, x_moment = real_basis(wide)
+    x_basis, x_moment = real_basis(space)
     yz = (moment.reshape(rows, 2, 1) + moment[None, None, :]).reshape(rows, LANES)
     yz = yz.astype(np.float32)
     plan = Plan(sizes, planes, rows, x_basis, x_moment)
@@ -846,10 +871,12 @@
     scratch += [vmem(*yz.shape), vmem(*source.shape), sems((12,))]
     scratch += [vmem(2 * ITERS, *plan.chunk)] * 2
     scratch += [sems((4 * ITERS, plan.groups, space)), vmem(len(plan.levels), 8, LANES)]
+    scratch += [vmem(*yz.shape), vmem(FIELDS, rows, LANES)]
     scratch += [vmem(*plan.slab)] * 2 + [vmem(54, planes, rows, LANES)]
     scratch += [vmem(18, planes + 1, rows, LANES), vmem(36, planes, rows, LANES)]
-    scratch += [vmem(ITERS, chunks, plan.ratio, rows, LANES)] * 2
-    scratch += [sems((ITERS, 4, chunks))]
+    scratch += [vmem(chunks, plan.ratio, rows, LANES)] * 2 + [sems((4, chunks))]
+    chunks = FIELDS * planes
+    scratch += [vmem(chunks, 1, rows, LANES)] * 2 + [sems((4, chunks))]
     scratch += [vmem(2 * pairs, 8, LANES), vmem(LANES, LANES), vmem(1, LANES)]
     final, table = pl.pallas_call(
         functools.partial(main_kernel, plan, stages),

time: 57.9 us -> 54.1 us (0.934)
  Pallas kernels: 55.2 us -> 51.4 us
    pallas_call x1, Pallas kernels: 53.4 us -> 49.5 us  [body(): pl.pallas_call(functools.partial(main_kernel, plan, stages), out_shape=[p...]
where the time goes in v3:
time: 54.1 us; the launch traced here: 53.9 us
  Pallas kernels  51.4 us (95%)
  between operations  2.58 us (5%)
    pallas_call x1, Pallas kernels, body(): pl.pallas_call(functools.partial(main_kernel, plan, stages), out_shape=[p...  49.5 us
    pallas_call x1, Pallas kernels, body(): pl.pallas_call(functools.partial(close_kernel, pairs, float(wide * area)...  1.83 us

profile of v3, /device:TPU:0, one launch (start us, length us, event | category | flops | bytes accessed | tf_op | source)
XLA Modules:
  0.0 53.9 jit_solution(11190359747445433527)
XLA Ops:
  2.6 49.5 %shard_map.113 = (f32[54,64,128]{2,1,0:T(8,128)S(1)}, f32[4,128]{1,0:T(4,128)S(1)}) custom-call(s32[1]{0:T(128)S(6)} %copy.15.sink_any, s32[1]{0:T(128)S(6)} %copy.16.src_any, s32[1]{0:T(128)S(6)} %copy.17.site_any, f32[54,64,128]{2,1,0:T(8,128)} %bitcast.16, bf16[384,256]{1,0:T(8,128)(2,1)} %constant.10.clone.right_any, ...), custom_call_target="tpu_custom_call" | custom-call | tf_op jit(solution)/shard_map/pallas_call | solution.py:881
  52.1 1.8 %shard_map.114 = (f32[54,64,128]{2,1,0:T(8,128)}, f32[2,144]{1,0:T(2,128)}) custom-call(f32[54,64,128]{2,1,0:T(8,128)S(1)} %get-tuple-element.6.final_ref, f32[4,128]{1,0:T(4,128)S(1)} %get-tuple-element.7.table_ref), custom_call_target="tpu_custom_call" | custom-call | tf_op jit(solution)/shard_map/pallas_call | solution.py:894

commit v4 on v3

--- a/solution.py
+++ b/solution.py
@@ -436,10 +436,10 @@
         send_ref[g, d, 1] = out[(d + 1) % n]
 
 
-def gauge_of(slab_ref, planes, gauge_ref):
+def gauge_of(slab_ref, planes, gauge_ref, chosen=None):
     rows = gauge_ref.shape[2]
 
-    for p in range(planes + 1):
+    for p in range(planes + 1) if chosen is None else chosen:
 
         @pl.loop(0, rows // 8)
         def _(j):
@@ -458,10 +458,10 @@
             ahead_ref[18 + e, p] = z_ahead(gauge_ref[e, p])
 
 
-def rotate_plane(get_band, put_band, p, gauge_ref, ahead_ref):
-    rows = gauge_ref.shape[2]
-
-    @pl.loop(0, rows // 8)
+def rotate_plane(get_band, put_band, p, gauge_ref, ahead_ref, part=0, parts=1):
+    bands = gauge_ref.shape[2] // 8
+
+    @pl.loop(part * bands // parts, (part + 1) * bands // parts)
     def _(j):
         start = pl.multiple_of(j * 8, 8)
         band = pl.ds(start, 8)
@@ -593,7 +593,7 @@
         Relay(times, sink_ref, own_one, up_one, down_one, sems_one),
         Relay(times, sink_ref, own_two, up_two, down_two, sems_two),
     ]
-    steps = [Steps(relays[0], 1.5, 0.7, 3.5), Steps(relays[1], 0.6, 0.35, 3.0)]
+    steps = [Steps(relays[0], 1.5, 0.7, 3.5), Steps(relays[1], 0.5, 0.35, 2.6)]
 
     def sweep(u, index, before=lambda: None):
         one, two = swaps[2 * index], swaps[2 * index + 1]
@@ -658,10 +658,11 @@
         steps[1].until(time[0])
 
     pause(0.0)
-    gauge_of(slab_two, planes, gauge_ref)
-    pause(0.7)
+    for p in range(planes + 1):
+        gauge_of(slab_two, planes, gauge_ref, [p])
+        pause(0.35)
     shift_all(planes, gauge_ref, ahead_ref)
-    pause(0.4)
+    pause(0.45)
 
     def get_last(i, r, a, b, p, j):
         return lattice_ref[i * 18 + at(r, a, b), p, pl.ds(pl.multiple_of(j * 8, 8), 8), :]
@@ -670,8 +671,9 @@
         out_ref[i * 18 + at(r, a, b), pl.ds(j * 8 * planes + p, 8, planes), :] = value
 
     for p in range(planes):
-        rotate_plane(get_last, put_last, p, gauge_ref, ahead_ref)
-        pause(0.7)
+        for part in range(2):
+            rotate_plane(get_last, put_last, p, gauge_ref, ahead_ref, part, 2)
+            pause(0.5)
     steps[0].until(1e9)
     for p in range(planes):
 
@@ -689,9 +691,11 @@
                     for part in range(2):
                         ahead_ref[at(part, a, b), p, band, :] = one[a][b][part]
 
-    pause(0.6)
+        pause(0.4)
+
     for swap in swaps:
         swap.drain()
+        pause(0.2)
     acc_ref[...] = jnp.zeros_like(acc_ref)
     sum_ref[...] = jnp.zeros_like(sum_ref)
     site = site_ref[0]

time: 54.1 us -> 53.6 us (level)
  Pallas kernels: 51.4 us -> 50.8 us
where the time goes in v4:
time: 53.6 us; the launch traced here: 53.4 us
  Pallas kernels  50.8 us (95%)
  between operations  2.58 us (5%)
    pallas_call x1, Pallas kernels, body(): pl.pallas_call(functools.partial(main_kernel, plan, stages), out_shape=[p...  49 us
    pallas_call x1, Pallas kernels, body(): pl.pallas_call(functools.partial(close_kernel, pairs, float(wide * area)...  1.83 us

profile of v4, /device:TPU:0, one launch (start us, length us, event | category | flops | bytes accessed | tf_op | source)
XLA Modules:
  0.0 53.4 jit_solution(9125486991737574941)
XLA Ops:
  2.6 49.0 %shard_map.113 = (f32[54,64,128]{2,1,0:T(8,128)S(1)}, f32[4,128]{1,0:T(4,128)S(1)}) custom-call(s32[1]{0:T(128)S(6)} %copy.15.sink_any, s32[1]{0:T(128)S(6)} %copy.16.src_any, s32[1]{0:T(128)S(6)} %copy.17.site_any, f32[54,64,128]{2,1,0:T(8,128)} %bitcast.16, bf16[384,256]{1,0:T(8,128)(2,1)} %constant.10.clone.right_any, ...), custom_call_target="tpu_custom_call" | custom-call | tf_op jit(solution)/shard_map/pallas_call | solution.py:885
  51.6 1.8 %shard_map.114 = (f32[54,64,128]{2,1,0:T(8,128)}, f32[2,144]{1,0:T(2,128)}) custom-call(f32[54,64,128]{2,1,0:T(8,128)S(1)} %get-tuple-element.6.final_ref, f32[4,128]{1,0:T(4,128)S(1)} %get-tuple-element.7.table_ref), custom_call_target="tpu_custom_call" | custom-call | tf_op jit(solution)/shard_map/pallas_call | solution.py:898
